TPU v7x, 32 devices: a whole 2x2x4 slice. The times are simulated.
32 devices in a mesh: dp: 8 (over z, x), shard: 4 (over y, core).
Axes of the slice: x: 2, y: 2, z: 4, core: 2. Of those that a mesh axis runs over, the one named last changes fastest.
Arguments:
- tokens: bfloat16 [128, 3584], P('dp', 'shard'), may hold values from -6 to 6
- targets: bfloat16 [128, 3584], P('dp', 'shard'), may hold values from -6 to 6
- task_of_token: int32 [128], P('dp'), may hold values from 0 to 15, never falling along the last dimension, each value on 1 to 16 neighbouring positions
- up_weight: bfloat16 [18944, 3584], P('dp', 'shard'), may hold values from -0.09375 to 0.09375
- down_weight: bfloat16 [18944, 3584], P('dp', 'shard'), may hold values from -0.046875 to 0.046875
- outer_up: bfloat16 [18944, 3584], P('dp', 'shard'), may hold values from -6 to 6
- outer_down: bfloat16 [18944, 3584], P('dp', 'shard'), may hold values from -6 to 6
Outputs:
- meta_up: float32 [18944, 3584], P('dp', 'shard')
- meta_down: float32 [18944, 3584], P('dp', 'shard')
Inputs may be any that keep to these rules, and one draw needn't show every extreme that they name: `task_of_token`: task numbers never fall along the tokens; every task has 1 to 16 tokens, and some task has exactly 16.
All inputs are finite; a program needn't handle non-finite values.
Results may differ from a plain program's by a relative error of at most 0.001.
Values may be sent and summed in bfloat16 or wider, within the bound.
A program may use at most 64 MiB of HBM per device.

v0:
```python
import jax
import jax.numpy as jnp
from jax import lax
from jax.sharding import PartitionSpec as P

TASKS = 16
ITERS = 2


def sigmoid_parts(linear_part):
    argument = linear_part.astype(jnp.float32)
    logistic = jax.nn.sigmoid(argument)
    derivative = logistic * (1.0 + argument * (1.0 - logistic))
    second_order = logistic * (1.0 - logistic) * (2.0 + argument * (1.0 - 2.0 * logistic))
    return (argument * logistic, derivative, second_order)


def contract_last(left_side, right_side):
    return lax.dot_general(
        left_side, right_side, (((1,), (1,)), ((), ())), preferred_element_type=jnp.float32
    )


def contract_first(left_side, right_side):
    return lax.dot_general(
        left_side, right_side, (((0,), (0,)), ((), ())), preferred_element_type=jnp.float32
    )


def over_hidden(partial_value):
    portion = lax.psum_scatter(
        partial_value.astype(jnp.bfloat16), "shard", scatter_dimension=1, tiled=True
    )
    return lax.all_gather(portion, "shard", axis=1, tiled=True)


def over_tokens(term_fn, row_count):
    return lax.psum_scatter(
        term_fn(jnp.int32(0), row_count * lax.axis_size("dp")).astype(jnp.bfloat16),
        "dp",
        scatter_dimension=0,
        tiled=True,
    ).astype(jnp.float32)


def all_tokens(local_part):
    return lax.all_gather(local_part, "dp", axis=0, tiled=True)


def paired_sum(first_up, second_up, first_down, second_down):
    return jnp.sum(first_up * second_up) + jnp.sum(first_down * second_down)


def both_totals(residual_up, residual_down, image_up, image_down):
    return lax.psum(
        (
            paired_sum(residual_up, residual_up, residual_down, residual_down),
            paired_sum(residual_up, image_up, residual_down, image_down),
        ),
        ("dp", "shard"),
    )


def body(tokens, targets, task_of_token, up_weight, down_weight, outer_up, outer_down):
    row_count = tokens.shape[0]
    task_index = jnp.arange(TASKS, dtype=jnp.int32)
    members = (task_of_token[:, None] == task_index[None, :]).astype(jnp.float32)
    task_counts = lax.psum(jnp.sum(members, axis=0), "dp")
    inverse = 1.0 / (TASKS * task_counts)
    weight = jnp.sum(members * inverse[None, :], axis=1)
    gathered = lax.all_gather(tokens, "dp", axis=0, tiled=True)
    linear_part = over_hidden(contract_last(gathered, up_weight))
    activation, derivative, second_order = sigmoid_parts(linear_part)
    hidden = activation.astype(jnp.bfloat16)

    def forward_term(first_row, slice_rows):
        return jnp.dot(hidden, down_weight, preferred_element_type=jnp.float32)

    output_rows = over_tokens(forward_term, row_count)
    errors = (weight[:, None] * (output_rows - targets.astype(jnp.float32))).astype(jnp.bfloat16)
    all_errors = all_tokens(errors)
    backward = over_hidden(contract_last(all_errors, down_weight)).astype(jnp.float32)

    def operator(vector_up, vector_down):
        direction_up = vector_up.astype(jnp.bfloat16)
        direction_down = vector_down.astype(jnp.bfloat16)
        tangent_linear = over_hidden(contract_last(gathered, direction_up)).astype(jnp.float32)
        tangent_hidden = (derivative * tangent_linear).astype(jnp.bfloat16)

        def tangent_term(first_row, slice_rows):
            return jnp.dot(
                tangent_hidden, down_weight, preferred_element_type=jnp.float32
            ) + jnp.dot(hidden, direction_down, preferred_element_type=jnp.float32)

        tangent_output = over_tokens(tangent_term, row_count)
        tangent_errors = (weight[:, None] * tangent_output).astype(jnp.bfloat16)
        gathered_tangent = all_tokens(tangent_errors)
        tangent_backward = over_hidden(
            contract_last(gathered_tangent, down_weight) + contract_last(all_errors, direction_down)
        )
        tangent_gate = (
            derivative * tangent_backward.astype(jnp.float32)
            + second_order * backward * tangent_linear
        ).astype(jnp.bfloat16)
        hessian_up = contract_first(tangent_gate, gathered)
        hessian_down = contract_first(tangent_hidden, all_errors) + contract_first(
            hidden, gathered_tangent
        )
        return (vector_up + hessian_up, vector_down + hessian_down)

    residual_up = outer_up.astype(jnp.float32)
    residual_down = outer_down.astype(jnp.float32)
    solution_up = jnp.zeros_like(residual_up)
    solution_down = jnp.zeros_like(residual_down)
    search_up, search_down = (residual_up, residual_down)
    image_up, image_down = operator(residual_up, residual_down)
    norm_now, product = both_totals(residual_up, residual_down, image_up, image_down)
    step_size = norm_now / product
    along_up, along_down = (image_up, image_down)
    for iteration in range(ITERS):
        solution_up = solution_up + step_size * search_up
        solution_down = solution_down + step_size * search_down
        residual_up = residual_up - step_size * along_up
        residual_down = residual_down - step_size * along_down
        if iteration + 1 < ITERS:
            image_up, image_down = operator(residual_up, residual_down)
            norm_next, product = both_totals(residual_up, residual_down, image_up, image_down)
            ratio_next = norm_next / norm_now
            step_size = norm_next / (product - ratio_next * norm_next / step_size)
            search_up = residual_up + ratio_next * search_up
            search_down = residual_down + ratio_next * search_down
            along_up = image_up + ratio_next * along_up
            along_down = image_down + ratio_next * along_down
            norm_now = norm_next
    return (solution_up, solution_down)


def solution(mesh):
    placed = (
        P("dp", "shard"),
        P("dp", "shard"),
        P("dp"),
        P("dp", "shard"),
        P("dp", "shard"),
        P("dp", "shard"),
        P("dp", "shard"),
    )
    return jax.shard_map(
        body,
        mesh=mesh,
        in_specs=placed,
        out_specs=(P("dp", "shard"), P("dp", "shard")),
        check_vma=False,
    )
```

profile of v0, /device:TPU:0, one launch (start us, length us, event | category | flops | bytes accessed | tf_op | source)
XLA Modules:
  0.0 610.7 jit_solution(8272210368168391806)
XLA Ops:
  7.2 32.7 %all_gather.30 = bf16[128,896]{1,0:T(8,128)(2,1)S(1)} all-gather(bf16[16,896]{1,0:T(8,128)(2,1)} %param.7), channel_id=1, replica_groups=mesh['dp'=8,'shard'=4] {'dp'}, dimensions={0}, use_global_device_ids=true | all-gather | bytes 258048 | tf_op jit(solution)/shard_map/all_gather | solution.py:71
  48.6 18.8 %reduce-scatter.10.cloned.1.call-done = bf16[128,592]{0,1:T(8,128)(2,1)} async-done(((bf16[128,2368]{0,1:T(8,128)(2,1)}), bf16[128,592]{0,1:T(8,128)(2,1)}) %reduce-scatter.10.cloned.1.call-update) | async-done | bytes 151568 | tf_op jit(solution)/shard_map/reduce_scatter | solution.py:31
  67.5 7.2 %all_gather.31 = bf16[128,2368]{0,1:T(8,128)(2,1)S(1)} all-gather(bf16[128,592]{0,1:T(8,128)(2,1)} %reduce-scatter.10.cloned.1.call-done), channel_id=1, replica_groups=mesh['dp'=8,'shard'=4] {'shard'}, dimensions={1}, use_global_device_ids=true | all-gather | bytes 757760 | tf_op jit(solution)/shard_map/all_gather | solution.py:34
  78.7 14.0 %reduce-scatter.12.cloned.1.call-done = bf16[128,592]{0,1:T(8,128)(2,1)} async-done(((bf16[128,2368]{0,1:T(8,128)(2,1)}), bf16[128,592]{0,1:T(8,128)(2,1)}) %reduce-scatter.12.cloned.1.call-update) | async-done | bytes 151568 | tf_op jit(solution)/shard_map/reduce_scatter | solution.py:31
  92.8 7.4 %all_gather.32 = bf16[128,2368]{0,1:T(8,128)(2,1)S(1)} all-gather(bf16[128,592]{0,1:T(8,128)(2,1)} %reduce-scatter.12.cloned.1.call-done), channel_id=1, replica_groups=mesh['dp'=8,'shard'=4] {'shard'}, dimensions={1}, use_global_device_ids=true | all-gather | bytes 757760 | tf_op jit(solution)/shard_map/all_gather | solution.py:34
  105.4 21.4 %psum.36 = f32[16]{0:T(128)S(1)} all-reduce(f32[16]{0:T(128)S(1)} %convert_reduce_fusion), channel_id=1, replica_groups=mesh['dp'=8,'shard'=4] {'dp'}, use_global_device_ids=true, to_apply=%region_5.0 | all-reduce | flops 16 | bytes 128 | tf_op jit(solution)/shard_map/psum | solution.py:68
  127.0 24.9 %reduce-scatter.16.cloned.1.call-done = bf16[16,896]{1,0:T(8,128)(2,1)} async-done(((bf16[128,896]{1,0:T(8,128)(2,1)}), bf16[16,896]{1,0:T(8,128)(2,1)}) %reduce-scatter.16.cloned.1.call-update) | async-done | bytes 28688 | tf_op jit(solution)/shard_map/reduce_scatter | solution.py:38
  151.8 57.9 %reduce-scatter.14.cloned.1.call-done = bf16[16,896]{1,0:T(8,128)(2,1)} async-done(((bf16[128,896]{1,0:T(8,128)(2,1)}), bf16[16,896]{1,0:T(8,128)(2,1)}) %reduce-scatter.14.cloned.1.call-update) | async-done | bytes 28688 | tf_op jit(solution)/shard_map/reduce_scatter | solution.py:38
  210.6 30.7 %all_gather.34 = bf16[128,896]{1,0:T(8,128)(2,1)S(1)} all-gather(bf16[16,896]{1,0:T(8,128)(2,1)S(1)} %get-tuple-element.10), channel_id=1, replica_groups=mesh['dp'=8,'shard'=4] {'dp'}, dimensions={0}, use_global_device_ids=true | all-gather | bytes 258048 | tf_op jit(solution)/shard_map/all_gather | solution.py:47
  245.7 30.7 %all_gather.33 = bf16[128,896]{1,0:T(8,128)(2,1)S(1)} all-gather(bf16[16,896]{1,0:T(8,128)(2,1)S(1)} %get-tuple-element.11), channel_id=1, replica_groups=mesh['dp'=8,'shard'=4] {'dp'}, dimensions={0}, use_global_device_ids=true | all-gather | bytes 258048 | tf_op jit(solution)/shard_map/all_gather | solution.py:47
  290.9 7.8 %all_gather.36 = bf16[128,2368]{0,1:T(8,128)(2,1)S(1)} all-gather(bf16[128,592]{0,1:T(8,128)(2,1)} %reduce-scatter.20.cloned.1.call-done), channel_id=1, replica_groups=mesh['dp'=8,'shard'=4] {'shard'}, dimensions={1}, use_global_device_ids=true | all-gather | bytes 757760 | tf_op jit(solution)/shard_map/all_gather | solution.py:34
  303.7 7.2 %all_gather.35 = bf16[128,2368]{0,1:T(8,128)(2,1)S(1)} all-gather(bf16[128,592]{0,1:T(8,128)(2,1)} %reduce-scatter.18.cloned.1.call-done), channel_id=1, replica_groups=mesh['dp'=8,'shard'=4] {'shard'}, dimensions={1}, use_global_device_ids=true | all-gather | bytes 757760 | tf_op jit(solution)/shard_map/all_gather | solution.py:34
  311.0 7.7 %fusion.3 = (f32[]{:T(128)}, f32[]{:T(128)}, f32[2368,896]{1,0:T(8,128)}) fusion(bf16[2368,896]{1,0:T(8,128)(2,1)} %param.12, bf16[128,896]{1,0:T(8,128)(2,1)S(1)} %all_gather.30, bf16[128,2368]{0,1:T(8,128)(2,1)S(1)} %all_gather.32, bf16[128,2368]{0,1:T(8,128)(2,1)S(1)} %all_gather.35, bf16[128,2368]{0,1:T(8,128)(2,1)S(1)} %all_gather.36, ...), kind=kOutput, calls=%fused_computation.17 | convolution fusion | flops 562561024 | bytes 15384584 | tf_op jit(solution)/shard_map/dot_general | solution.py:25
  321.2 39.9 %all-reduce.1 = (f32[]{:T(128)}, f32[]{:T(128)}) all-reduce(f32[]{:T(128)S(6)} %add.97, f32[]{:T(128)S(6)} %add.107), channel_id=1, replica_groups=mesh['dp'=8,'shard'=4] {'dp','shard'}, use_global_device_ids=true, to_apply=%region_2.0 | all-reduce | flops 2 | bytes 16 | tf_op jit(solution)/shard_map/psum | solution.py:55
  369.4 7.4 %multiply_reduce_fusion.1 = f32[]{:T(128)} fusion(f32[2368,896]{1,0:T(8,128)} %get-tuple-element.12, f32[]{:T(128)S(6)} %div.20, bf16[2368,896]{1,0:T(8,128)(2,1)} %param.12), kind=kLoop, calls=%fused_computation.27 | loop fusion | flops 12730367 | bytes 12730376 | tf_op jit(solution)/shard_map/reduce_sum | solution.py:51
  376.7 15.2 %reduce-scatter.22.cloned.1.call-done = bf16[128,592]{0,1:T(8,128)(2,1)} async-done(((bf16[128,2368]{0,1:T(8,128)(2,1)}), bf16[128,592]{0,1:T(8,128)(2,1)}) %reduce-scatter.22.cloned.1.call-update) | async-done | bytes 151568 | tf_op jit(solution)/shard_map/reduce_scatter | solution.py:31
  392.0 7.5 %all_gather.37 = bf16[128,2368]{0,1:T(8,128)(2,1)S(1)} all-gather(bf16[128,592]{0,1:T(8,128)(2,1)} %reduce-scatter.22.cloned.1.call-done), channel_id=1, replica_groups=mesh['dp'=8,'shard'=4] {'shard'}, dimensions={1}, use_global_device_ids=true | all-gather | bytes 757760 | tf_op jit(solution)/shard_map/all_gather | solution.py:34
  410.0 7.5 %multiply_reduce_fusion = f32[]{:T(128)} fusion(f32[2368,896]{1,0:T(8,128)} %get-tuple-element.13, f32[]{:T(128)S(6)} %div.20, bf16[2368,896]{1,0:T(8,128)(2,1)} %param.13), kind=kLoop, calls=%fused_computation.26 | loop fusion | flops 10608639 | bytes 12730376 | tf_op jit(solution)/shard_map/reduce_sum | solution.py:51
  418.6 47.3 %reduce-scatter.24.cloned.1.call-done = bf16[16,896]{1,0:T(8,128)(2,1)} async-done(((bf16[128,896]{1,0:T(8,128)(2,1)}), bf16[16,896]{1,0:T(8,128)(2,1)}) %reduce-scatter.24.cloned.1.call-update) | async-done | bytes 28688 | tf_op jit(solution)/shard_map/reduce_scatter | solution.py:38
  466.7 30.7 %all_gather.38 = bf16[128,896]{1,0:T(8,128)(2,1)S(1)} all-gather(bf16[16,896]{1,0:T(8,128)(2,1)S(1)} %multiply_convert_fusion), channel_id=1, replica_groups=mesh['dp'=8,'shard'=4] {'dp'}, dimensions={0}, use_global_device_ids=true | all-gather | bytes 258048 | tf_op jit(solution)/shard_map/all_gather | solution.py:47
  515.9 13.5 %reduce-scatter.26.cloned.1.call-done = bf16[128,592]{0,1:T(8,128)(2,1)} async-done(((bf16[128,2368]{0,1:T(8,128)(2,1)}), bf16[128,592]{0,1:T(8,128)(2,1)}) %reduce-scatter.26.cloned.1.call-update) | async-done | bytes 151568 | tf_op jit(solution)/shard_map/reduce_scatter | solution.py:31
  529.3 7.5 %all_gather.39 = bf16[128,2368]{0,1:T(8,128)(2,1)S(1)} all-gather(bf16[128,592]{0,1:T(8,128)(2,1)} %reduce-scatter.26.cloned.1.call-done), channel_id=1, replica_groups=mesh['dp'=8,'shard'=4] {'shard'}, dimensions={1}, use_global_device_ids=true | all-gather | bytes 757760 | tf_op jit(solution)/shard_map/all_gather | solution.py:34
  545.0 39.9 %all-reduce = (f32[]{:T(128)}, f32[]{:T(128)}) all-reduce(f32[]{:T(128)S(6)} %add.108, f32[]{:T(128)S(6)} %add.115), channel_id=1, replica_groups=mesh['dp'=8,'shard'=4] {'dp','shard'}, use_global_device_ids=true, to_apply=%region_17.0 | all-reduce | flops 2 | bytes 16 | tf_op jit(solution)/shard_map/psum | solution.py:55
  589.3 14.8 %fusion.4 = (f32[2368,896]{1,0:T(8,128)}, f32[2368,896]{1,0:T(8,128)}) fusion(bf16[2368,896]{1,0:T(8,128)(2,1)} %param.12, f32[]{:T(128)S(6)} %div.21, f32[]{:T(128)S(6)} %div.23, f32[]{:T(128)S(6)} %div.20, f32[2368,896]{1,0:T(8,128)} %get-tuple-element.12, f32[2368,896]{1,0:T(8,128)} %get-tuple-element.13, bf16[2368,896]{1,0:T(8,128)(2,1)} %param.13), kind=kLoop, calls=%fused_computation.18 | loop fusion | flops 36069376 | bytes 42434572 | tf_op jit(solution)/shard_map/add | solution.py:121
  (57 shorter events, 86.5 us)
Async XLA Ops:
  7.2 60.3 %reduce-scatter.10.cloned.1.call-start = ((), (), s32[]{:S(2)}) async-start(), calls=%async_computation.9 | async-start | bytes 757760 | tf_op jit(solution)/shard_map/reduce_scatter | solution.py:31
  44.2 48.5 %reduce-scatter.12.cloned.1.call-start = ((), (), s32[]{:S(2)}) async-start(), calls=%async_computation.10 | async-start | bytes 757760 | tf_op jit(solution)/shard_map/reduce_scatter | solution.py:31
  48.6 103.2 %reduce-scatter.16.cloned.1.call-start = ((), (), s32[]{:S(2)}) async-start(), calls=%async_computation.12 | async-start | bytes 258048 | tf_op jit(solution)/shard_map/reduce_scatter | solution.py:38
  78.7 131.1 %reduce-scatter.14.cloned.1.call-start = ((), (), s32[]{:S(2)}) async-start(), calls=%async_computation.11 | async-start | bytes 258048 | tf_op jit(solution)/shard_map/reduce_scatter | solution.py:38
  92.8 10.8 %slice-start = ((s8[4243456]{0:T(1024)(128)(4,1)}), s8[4194304]{0:T(1024)(128)(4,1)S(1)}, s32[]{:S(2)}) async-start(s8[4243456]{0:T(1024)(128)(4,1)} %bitcast.26), calls=%async_computation.18 | async-start | bytes 8388608
  100.1 3.4 slice-start.1
  103.5 1.8 copy-start.1
  103.5 106.2 %copy-start = (bf16[16,896]{1,0:T(8,128)(2,1)S(1)}, bf16[16,896]{1,0:T(8,128)(2,1)}, u32[]{:S(2)}) copy-start(bf16[16,896]{1,0:T(8,128)(2,1)} %param.8) | copy-start | bytes 86020
  105.2 185.7 %reduce-scatter.20.cloned.1.call-start = ((), (), s32[]{:S(2)}) async-start(), calls=%async_computation.14 | async-start | bytes 757760 | tf_op jit(solution)/shard_map/reduce_scatter | solution.py:31
  245.6 34.4 %slice-start.2 = ((s8[4243456]{0:T(1024)(128)(4,1)}), s8[49152]{0:T(1024)(128)(4,1)S(1)}, s32[]{:S(2)}) async-start(s8[4243456]{0:T(1024)(128)(4,1)} %bitcast.28), calls=%async_computation.20 | async-start | bytes 98304
  245.7 58.1 %reduce-scatter.18.cloned.1.call-start = ((), (), s32[]{:S(2)}) async-start(), calls=%async_computation.13 | async-start | bytes 757760 | tf_op jit(solution)/shard_map/reduce_scatter | solution.py:31
  276.4 3.7 slice-start.3
  282.2 109.8 %reduce-scatter.22.cloned.1.call-start = ((), (), s32[]{:S(2)}) async-start(), calls=%async_computation.15 | async-start | bytes 757760 | tf_op jit(solution)/shard_map/reduce_scatter | solution.py:31
  369.3 96.6 %reduce-scatter.24.cloned.1.call-start = ((), (), s32[]{:S(2)}) async-start(), calls=%async_computation.16 | async-start | bytes 258048 | tf_op jit(solution)/shard_map/reduce_scatter | solution.py:38
  409.9 119.4 %reduce-scatter.26.cloned.1.call-start = ((), (), s32[]{:S(2)}) async-start(), calls=%async_computation.17 | async-start | bytes 757760 | tf_op jit(solution)/shard_map/reduce_scatter | solution.py:31
Sparse Core Ops, SparseCore 0:
  44.4 23.0 reduce-scatter.9
  70.6 22.1 reduce-scatter.11
  96.5 55.2 reduce-scatter.15
  155.4 54.3 reduce-scatter.13
  245.8 21.3 reduce-scatter.19
  282.3 21.3 reduce-scatter.17
  369.4 22.5 reduce-scatter.21
  410.1 55.8 reduce-scatter.23
  508.0 21.3 reduce-scatter.25
where the time goes:
time: 612 us; the launch traced here: 611 us
  blocking collectives  271 us (44%)
  waiting for transfers between devices  197 us (32%)
  matrix products  86.5 us (14%)
  other arithmetic  31.6 us (5%)
  between operations  24.6 us (4%)
    reduce_scatter x3, waiting for transfers between devices, over_tokens(): lax.psum_scatter(term_fn(jnp.int32(0), row_count * lax.axis_size('dp')).a...  130 us
    all_gather x3, blocking collectives, all_tokens(): return lax.all_gather(local_part, 'dp', axis=0, tiled=True)  92.1 us
    psum x2, blocking collectives, both_totals(): lax.psum((paired_sum(residual_up, residual_up, residual_down, residual_do...  79.7 us
    reduce_scatter x6, waiting for transfers between devices, over_hidden(): lax.psum_scatter(partial_value.astype(jnp.bfloat16), 'shard', scatter_dim...  66.6 us
    all_gather x6, blocking collectives, over_hidden(): return lax.all_gather(portion, 'shard', axis=1, tiled=True)  44.6 us
    dot_general x8, matrix products, contract_last(): lax.dot_general(left_side, right_side, (((1,), (1,)), ((), ())), preferre...  35.9 us
    all_gather x1, blocking collectives, body(): gathered = lax.all_gather(tokens, 'dp', axis=0, tiled=True)  32.7 us
    dot_general x6, matrix products, contract_first(): lax.dot_general(left_side, right_side, (((0,), (0,)), ((), ())), preferre...  31.2 us
  transfers between devices with their start and end apart: 9, of which 8 were waited for; matrix products, arithmetic and copies ran while one was open for 8% of the time, Pallas kernels for 0%

commit v1 on v0

--- a/solution.py
+++ b/solution.py
@@ -5,6 +5,10 @@
 
 TASKS = 16
 ITERS = 2
+
+
+def edge_pack(own_rows, dev_axis, group_axis):
+    return lax.psum(lax.psum(own_rows, dev_axis), group_axis)
 
 
 def sigmoid_parts(linear_part):
@@ -52,12 +56,13 @@
 
 
 def both_totals(residual_up, residual_down, image_up, image_down):
-    return lax.psum(
+    return edge_pack(
         (
             paired_sum(residual_up, residual_up, residual_down, residual_down),
             paired_sum(residual_up, image_up, residual_down, image_down),
         ),
-        ("dp", "shard"),
+        dev_axis="shard",
+        group_axis="dp",
     )
 
 

time: 612 us -> 587 us (0.959)
  blocking collectives: 271 us -> 249 us
    psum x2 -> x4, blocking collectives: 79.7 us -> 58.9 us  [edge_pack(): return lax.psum(lax.psum(own_rows, dev_axis), group_axis)]
  transfers between devices with their start and end apart: 9 -> 9, of which waited for: 8 -> 8; matrix products, arithmetic and copies ran while one was open for 8% -> 9% of each run, Pallas kernels for 0% -> 0%
where the time goes in v1:
time: 587 us; the launch traced here: 586 us
  blocking collectives  249 us (42%)
  waiting for transfers between devices  193 us (33%)
  matrix products  86.5 us (15%)
  other arithmetic  31.8 us (5%)
  between operations  24.6 us (4%)
    reduce_scatter x3, waiting for transfers between devices, over_tokens(): lax.psum_scatter(term_fn(jnp.int32(0), row_count * lax.axis_size('dp')).a...  130 us
    all_gather x3, blocking collectives, all_tokens(): return lax.all_gather(local_part, 'dp', axis=0, tiled=True)  92.1 us
    reduce_scatter x6, waiting for transfers between devices, over_hidden(): lax.psum_scatter(partial_value.astype(jnp.bfloat16), 'shard', scatter_dim...  62.7 us
    psum x4, blocking collectives, edge_pack(): return lax.psum(lax.psum(own_rows, dev_axis), group_axis)  58.9 us
    all_gather x6, blocking collectives, over_hidden(): return lax.all_gather(portion, 'shard', axis=1, tiled=True)  44.1 us
    dot_general x8, matrix products, contract_last(): lax.dot_general(left_side, right_side, (((1,), (1,)), ((), ())), preferre...  35.9 us
    all_gather x1, blocking collectives, body(): gathered = lax.all_gather(tokens, 'dp', axis=0, tiled=True)  32.7 us
    dot_general x6, matrix products, contract_first(): lax.dot_general(left_side, right_side, (((0,), (0,)), ((), ())), preferre...  31.2 us
  transfers between devices with their start and end apart: 9, of which 8 were waited for; matrix products, arithmetic and copies ran while one was open for 9% of the time, Pallas kernels for 0%

profile of v1, /device:TPU:0, one launch (start us, length us, event | category | flops | bytes accessed | tf_op | source)
XLA Modules:
  0.0 585.7 jit_solution(6819534795907611993)
XLA Ops:
  7.2 32.7 %all_gather.30 = bf16[128,896]{1,0:T(8,128)(2,1)S(1)} all-gather(bf16[16,896]{1,0:T(8,128)(2,1)} %param.7), channel_id=1, replica_groups=mesh['dp'=8,'shard'=4] {'dp'}, dimensions={0}, use_global_device_ids=true | all-gather | bytes 258048 | tf_op jit(solution)/shard_map/all_gather | solution.py:76
  48.6 18.8 %reduce-scatter.10.cloned.1.call-done = bf16[128,592]{0,1:T(8,128)(2,1)} async-done(((bf16[128,2368]{0,1:T(8,128)(2,1)}), bf16[128,592]{0,1:T(8,128)(2,1)}) %reduce-scatter.10.cloned.1.call-update) | async-done | bytes 151568 | tf_op jit(solution)/shard_map/reduce_scatter | solution.py:35
  78.7 14.0 %reduce-scatter.12.cloned.1.call-done = bf16[128,592]{0,1:T(8,128)(2,1)} async-done(((bf16[128,2368]{0,1:T(8,128)(2,1)}), bf16[128,592]{0,1:T(8,128)(2,1)}) %reduce-scatter.12.cloned.1.call-update) | async-done | bytes 151568 | tf_op jit(solution)/shard_map/reduce_scatter | solution.py:35
  92.8 7.4 %all_gather.32 = bf16[128,2368]{0,1:T(8,128)(2,1)S(1)} all-gather(bf16[128,592]{0,1:T(8,128)(2,1)} %reduce-scatter.12.cloned.1.call-done), channel_id=1, replica_groups=mesh['dp'=8,'shard'=4] {'shard'}, dimensions={1}, use_global_device_ids=true | all-gather | bytes 757760 | tf_op jit(solution)/shard_map/all_gather | solution.py:38
  105.4 21.4 %psum.65 = f32[16]{0:T(128)S(1)} all-reduce(f32[16]{0:T(128)S(1)} %convert_reduce_fusion), channel_id=1, replica_groups=mesh['dp'=8,'shard'=4] {'dp'}, use_global_device_ids=true, to_apply=%region_6.0 | all-reduce | flops 16 | bytes 128 | tf_op jit(solution)/shard_map/psum | solution.py:73
  127.0 24.9 %reduce-scatter.16.cloned.1.call-done = bf16[16,896]{1,0:T(8,128)(2,1)} async-done(((bf16[128,896]{1,0:T(8,128)(2,1)}), bf16[16,896]{1,0:T(8,128)(2,1)}) %reduce-scatter.16.cloned.1.call-update) | async-done | bytes 28688 | tf_op jit(solution)/shard_map/reduce_scatter | solution.py:42
  151.8 57.9 %reduce-scatter.14.cloned.1.call-done = bf16[16,896]{1,0:T(8,128)(2,1)} async-done(((bf16[128,896]{1,0:T(8,128)(2,1)}), bf16[16,896]{1,0:T(8,128)(2,1)}) %reduce-scatter.14.cloned.1.call-update) | async-done | bytes 28688 | tf_op jit(solution)/shard_map/reduce_scatter | solution.py:42
  210.6 30.7 %all_gather.34 = bf16[128,896]{1,0:T(8,128)(2,1)S(1)} all-gather(bf16[16,896]{1,0:T(8,128)(2,1)S(1)} %get-tuple-element.14), channel_id=1, replica_groups=mesh['dp'=8,'shard'=4] {'dp'}, dimensions={0}, use_global_device_ids=true | all-gather | bytes 258048 | tf_op jit(solution)/shard_map/all_gather | solution.py:51
  245.7 30.7 %all_gather.33 = bf16[128,896]{1,0:T(8,128)(2,1)S(1)} all-gather(bf16[16,896]{1,0:T(8,128)(2,1)S(1)} %get-tuple-element.15), channel_id=1, replica_groups=mesh['dp'=8,'shard'=4] {'dp'}, dimensions={0}, use_global_device_ids=true | all-gather | bytes 258048 | tf_op jit(solution)/shard_map/all_gather | solution.py:51
  290.9 7.8 %all_gather.36 = bf16[128,2368]{0,1:T(8,128)(2,1)S(1)} all-gather(bf16[128,592]{0,1:T(8,128)(2,1)} %reduce-scatter.20.cloned.1.call-done), channel_id=1, replica_groups=mesh['dp'=8,'shard'=4] {'shard'}, dimensions={1}, use_global_device_ids=true | all-gather | bytes 757760 | tf_op jit(solution)/shard_map/all_gather | solution.py:38
  303.7 7.2 %all_gather.35 = bf16[128,2368]{0,1:T(8,128)(2,1)S(1)} all-gather(bf16[128,592]{0,1:T(8,128)(2,1)} %reduce-scatter.18.cloned.1.call-done), channel_id=1, replica_groups=mesh['dp'=8,'shard'=4] {'shard'}, dimensions={1}, use_global_device_ids=true | all-gather | bytes 757760 | tf_op jit(solution)/shard_map/all_gather | solution.py:38
  311.0 7.7 %fusion.3 = (f32[]{:T(128)}, f32[]{:T(128)}, f32[2368,896]{1,0:T(8,128)}) fusion(bf16[2368,896]{1,0:T(8,128)(2,1)} %param.12, bf16[128,896]{1,0:T(8,128)(2,1)S(1)} %all_gather.30, bf16[128,2368]{0,1:T(8,128)(2,1)S(1)} %all_gather.32, bf16[128,2368]{0,1:T(8,128)(2,1)S(1)} %all_gather.35, bf16[128,2368]{0,1:T(8,128)(2,1)S(1)} %all_gather.36, ...), kind=kOutput, calls=%fused_computation.17 | convolution fusion | flops 562561024 | bytes 15384584 | tf_op jit(solution)/shard_map/dot_general | solution.py:29
  321.2 7.3 %all-reduce.3 = (f32[]{:T(128)}, f32[]{:T(128)}) all-reduce(f32[]{:T(128)S(6)} %add.105, f32[]{:T(128)S(6)} %add.115), channel_id=1, replica_groups=mesh['dp'=8,'shard'=4] {'shard'}, use_global_device_ids=true, to_apply=%region_2.0 | all-reduce | flops 2 | bytes 16 | tf_op jit(solution)/shard_map/psum | solution.py:11
  328.5 22.0 %all-reduce.1 = (f32[]{:T(128)}, f32[]{:T(128)}) all-reduce(f32[]{:T(128)} %get-tuple-element.12, f32[]{:T(128)} %get-tuple-element.13), channel_id=1, replica_groups=mesh['dp'=8,'shard'=4] {'dp'}, use_global_device_ids=true, to_apply=%region_3.0 | all-reduce | flops 2 | bytes 16 | tf_op jit(solution)/shard_map/psum | solution.py:11
  358.8 7.6 %multiply_reduce_fusion.1 = f32[]{:T(128)} fusion(f32[2368,896]{1,0:T(8,128)} %get-tuple-element.16, f32[]{:T(128)S(6)} %div.20, bf16[2368,896]{1,0:T(8,128)(2,1)} %param.12), kind=kLoop, calls=%fused_computation.27 | loop fusion | flops 12730367 | bytes 12730376 | tf_op jit(solution)/shard_map/reduce_sum | solution.py:55
  366.5 11.3 %reduce-scatter.22.cloned.1.call-done = bf16[128,592]{0,1:T(8,128)(2,1)} async-done(((bf16[128,2368]{0,1:T(8,128)(2,1)}), bf16[128,592]{0,1:T(8,128)(2,1)}) %reduce-scatter.22.cloned.1.call-update) | async-done | bytes 151568 | tf_op jit(solution)/shard_map/reduce_scatter | solution.py:35
  377.8 7.2 %all_gather.37 = bf16[128,2368]{0,1:T(8,128)(2,1)S(1)} all-gather(bf16[128,592]{0,1:T(8,128)(2,1)} %reduce-scatter.22.cloned.1.call-done), channel_id=1, replica_groups=mesh['dp'=8,'shard'=4] {'shard'}, dimensions={1}, use_global_device_ids=true | all-gather | bytes 757760 | tf_op jit(solution)/shard_map/all_gather | solution.py:38
  395.8 7.5 %multiply_reduce_fusion = f32[]{:T(128)} fusion(f32[2368,896]{1,0:T(8,128)} %get-tuple-element.17, f32[]{:T(128)S(6)} %div.20, bf16[2368,896]{1,0:T(8,128)(2,1)} %param.13), kind=kLoop, calls=%fused_computation.26 | loop fusion | flops 10608639 | bytes 12730376 | tf_op jit(solution)/shard_map/reduce_sum | solution.py:55
  404.4 47.1 %reduce-scatter.24.cloned.1.call-done = bf16[16,896]{1,0:T(8,128)(2,1)} async-done(((bf16[128,896]{1,0:T(8,128)(2,1)}), bf16[16,896]{1,0:T(8,128)(2,1)}) %reduce-scatter.24.cloned.1.call-update) | async-done | bytes 28688 | tf_op jit(solution)/shard_map/reduce_scatter | solution.py:42
  452.4 30.7 %all_gather.38 = bf16[128,896]{1,0:T(8,128)(2,1)S(1)} all-gather(bf16[16,896]{1,0:T(8,128)(2,1)S(1)} %multiply_convert_fusion), channel_id=1, replica_groups=mesh['dp'=8,'shard'=4] {'dp'}, dimensions={0}, use_global_device_ids=true | all-gather | bytes 258048 | tf_op jit(solution)/shard_map/all_gather | solution.py:51
  501.5 13.5 %reduce-scatter.26.cloned.1.call-done = bf16[128,592]{0,1:T(8,128)(2,1)} async-done(((bf16[128,2368]{0,1:T(8,128)(2,1)}), bf16[128,592]{0,1:T(8,128)(2,1)}) %reduce-scatter.26.cloned.1.call-update) | async-done | bytes 151568 | tf_op jit(solution)/shard_map/reduce_scatter | solution.py:35
  530.4 7.3 %all-reduce.2 = (f32[]{:T(128)}, f32[]{:T(128)}) all-reduce(f32[]{:T(128)S(6)} %add.116, f32[]{:T(128)S(6)} %add.123), channel_id=1, replica_groups=mesh['dp'=8,'shard'=4] {'shard'}, use_global_device_ids=true, to_apply=%region_19.0 | all-reduce | flops 2 | bytes 16 | tf_op jit(solution)/shard_map/psum | solution.py:11
  537.7 22.3 %all-reduce = (f32[]{:T(128)}, f32[]{:T(128)}) all-reduce(f32[]{:T(128)} %get-tuple-element.10, f32[]{:T(128)} %get-tuple-element.11), channel_id=1, replica_groups=mesh['dp'=8,'shard'=4] {'dp'}, use_global_device_ids=true, to_apply=%region_20.0 | all-reduce | flops 2 | bytes 16 | tf_op jit(solution)/shard_map/psum | solution.py:11
  564.4 14.8 %fusion.4 = (f32[2368,896]{1,0:T(8,128)}, f32[2368,896]{1,0:T(8,128)}) fusion(bf16[2368,896]{1,0:T(8,128)(2,1)} %param.12, f32[]{:T(128)S(6)} %div.21, f32[]{:T(128)S(6)} %div.23, f32[]{:T(128)S(6)} %div.20, f32[2368,896]{1,0:T(8,128)} %get-tuple-element.16, f32[2368,896]{1,0:T(8,128)} %get-tuple-element.17, bf16[2368,896]{1,0:T(8,128)(2,1)} %param.13), kind=kLoop, calls=%fused_computation.18 | loop fusion | flops 36069376 | bytes 42434572 | tf_op jit(solution)/shard_map/add | solution.py:126
  (59 shorter events, 101.2 us)
Async XLA Ops:
  7.2 60.3 %reduce-scatter.10.cloned.1.call-start = ((), (), s32[]{:S(2)}) async-start(), calls=%async_computation.9 | async-start | bytes 757760 | tf_op jit(solution)/shard_map/reduce_scatter | solution.py:35
  44.2 48.5 %reduce-scatter.12.cloned.1.call-start = ((), (), s32[]{:S(2)}) async-start(), calls=%async_computation.10 | async-start | bytes 757760 | tf_op jit(solution)/shard_map/reduce_scatter | solution.py:35
  48.6 103.2 %reduce-scatter.16.cloned.1.call-start = ((), (), s32[]{:S(2)}) async-start(), calls=%async_computation.12 | async-start | bytes 258048 | tf_op jit(solution)/shard_map/reduce_scatter | solution.py:42
  78.7 131.1 %reduce-scatter.14.cloned.1.call-start = ((), (), s32[]{:S(2)}) async-start(), calls=%async_computation.11 | async-start | bytes 258048 | tf_op jit(solution)/shard_map/reduce_scatter | solution.py:42
  92.8 10.8 %slice-start = ((s8[4243456]{0:T(1024)(128)(4,1)}), s8[4194304]{0:T(1024)(128)(4,1)S(1)}, s32[]{:S(2)}) async-start(s8[4243456]{0:T(1024)(128)(4,1)} %bitcast.26), calls=%async_computation.18 | async-start | bytes 8388608
  100.1 3.4 slice-start.1
  103.5 1.8 copy-start.1
  103.5 106.2 %copy-start = (bf16[16,896]{1,0:T(8,128)(2,1)S(1)}, bf16[16,896]{1,0:T(8,128)(2,1)}, u32[]{:S(2)}) copy-start(bf16[16,896]{1,0:T(8,128)(2,1)} %param.8) | copy-start | bytes 86020
  105.2 185.7 %reduce-scatter.20.cloned.1.call-start = ((), (), s32[]{:S(2)}) async-start(), calls=%async_computation.14 | async-start | bytes 757760 | tf_op jit(solution)/shard_map/reduce_scatter | solution.py:35
  245.6 34.4 %slice-start.2 = ((s8[4243456]{0:T(1024)(128)(4,1)}), s8[49152]{0:T(1024)(128)(4,1)S(1)}, s32[]{:S(2)}) async-start(s8[4243456]{0:T(1024)(128)(4,1)} %bitcast.28), calls=%async_computation.20 | async-start | bytes 98304
  245.7 58.1 %reduce-scatter.18.cloned.1.call-start = ((), (), s32[]{:S(2)}) async-start(), calls=%async_computation.13 | async-start | bytes 757760 | tf_op jit(solution)/shard_map/reduce_scatter | solution.py:35
  276.4 3.7 slice-start.3
  282.2 95.6 %reduce-scatter.22.cloned.1.call-start = ((), (), s32[]{:S(2)}) async-start(), calls=%async_computation.15 | async-start | bytes 757760 | tf_op jit(solution)/shard_map/reduce_scatter | solution.py:35
  358.8 92.7 %reduce-scatter.24.cloned.1.call-start = ((), (), s32[]{:S(2)}) async-start(), calls=%async_computation.16 | async-start | bytes 258048 | tf_op jit(solution)/shard_map/reduce_scatter | solution.py:42
  395.5 119.4 %reduce-scatter.26.cloned.1.call-start = ((), (), s32[]{:S(2)}) async-start(), calls=%async_computation.17 | async-start | bytes 757760 | tf_op jit(solution)/shard_map/reduce_scatter | solution.py:35
Sparse Core Ops, SparseCore 0:
  44.4 23.0 reduce-scatter.9
  70.6 22.1 reduce-scatter.11
  96.5 55.2 reduce-scatter.15
  155.4 54.3 reduce-scatter.13
  245.8 21.3 reduce-scatter.19
  282.3 21.3 reduce-scatter.17
  358.9 18.8 reduce-scatter.21
  395.6 55.8 reduce-scatter.23
  493.5 21.3 reduce-scatter.25
